TPU v7x, 32 devices: a whole 2x2x4 slice. The times are simulated.
32 devices in a mesh: dap: 16 (over z, y, x), dp: 2 (over core).
Axes of the slice: x: 2, y: 2, z: 4, core: 2. Of those that a mesh axis runs over, the one named last changes fastest.
Arguments:
- edge_embedding: bfloat16 [192, 96, 128], P(('dp', 'dap')), parts along dimension 0, may hold values from -6 to 6
- alignment_embedding: bfloat16 [128, 96, 256], P('dp', 'dap'), parts along dimension 0, may hold values from -6 to 6
- tensor_flank_matrix: bfloat16 [256, 64], replicated, may hold values from -0.375 to 0.375
- tensor_final_matrix: bfloat16 [1024, 128], replicated, may hold values from -0.75 to 0.75
- outward_sigmoid_matrix: bfloat16 [128, 640], replicated, may hold values from -0.5 to 0.5
- outward_final_matrix: bfloat16 [128, 128], replicated, may hold values from -0.5 to 0.5
- inward_sigmoid_matrix: bfloat16 [128, 640], replicated, may hold values from -0.5 to 0.5
- inward_final_matrix: bfloat16 [128, 128], replicated, may hold values from -0.5 to 0.5
- adjoint_seed: bfloat16 [192, 96, 128], P(('dp', 'dap')), parts along dimension 0, may hold values from -6 to 6
Outputs:
- edge_embedding_updated: bfloat16 [192, 96, 128], P(('dp', 'dap')), parts along dimension 0
- edge_embedding_adjoint: bfloat16 [192, 96, 128], P(('dp', 'dap')), parts along dimension 0
- alignment_adjoint: bfloat16 [128, 96, 256], P('dp', 'dap'), parts along dimension 0
- outer_proj_grad: float32 [512, 64], P('dp'), parts along dimension 0
- outer_final_grad: float32 [2048, 128], P('dp'), parts along dimension 0
- outgoing_proj_grad: float32 [256, 640], P('dp'), parts along dimension 0
- outgoing_final_grad: float32 [256, 128], P('dp'), parts along dimension 0
- incoming_proj_grad: float32 [256, 640], P('dp'), parts along dimension 0
- incoming_final_grad: float32 [256, 128], P('dp'), parts along dimension 0
There are 2 independent parts, one for each index of `dp`. A program takes and returns all parts, laid end to end along the dimension named above; an argument that names none is the same for every part. Nothing has to cross between parts.
All inputs are finite; a program needn't handle non-finite values.
Results may differ from a plain program's by a relative error of at most 0.02.
Values may be sent and summed in bfloat16 or wider, within the bound.
No kernel may reach another device: no remote copies, remote signals or barrier semaphores. Data moves between devices by JAX's collectives and lax.ppermute only.
A program may use at most 128 MiB of HBM per device.

v0:
```python
import jax
import jax.numpy as jnp
from jax import lax
from jax.sharding import PartitionSpec as P

EPSILON = 1e-05


def truncated_numbers(values):
    return lax.optimization_barrier(values.astype(jnp.bfloat16))


def edge_standardized(values, which_axis):
    average = jnp.mean(values, axis=which_axis, keepdims=True)
    centred = values - average
    factor = lax.rsqrt(jnp.mean(centred * centred, axis=which_axis, keepdims=True) + EPSILON)
    return centred * factor


def standardizer_adjoint(values, gradient, which_axis):
    average = jnp.mean(values, axis=which_axis, keepdims=True)
    centred = values - average
    factor = lax.rsqrt(jnp.mean(centred * centred, axis=which_axis, keepdims=True) + EPSILON)
    hatted = centred * factor
    return factor * (
        gradient
        - jnp.mean(gradient, axis=which_axis, keepdims=True)
        - hatted * jnp.mean(gradient * hatted, axis=which_axis, keepdims=True)
    )


def sigmoid_pieces(edge_entry, linear_mapping, latent_tensor):
    standardized_edges = truncated_numbers(edge_standardized(edge_entry.astype(jnp.float32), 2))
    gate_pre = jnp.dot(
        standardized_edges,
        linear_mapping[:, 4 * latent_tensor :],
        preferred_element_type=jnp.float32,
    )
    split_pre = jnp.einsum(
        "rnz,zc->crn",
        standardized_edges,
        linear_mapping[:, : 4 * latent_tensor],
        preferred_element_type=jnp.float32,
    )
    source_masked = truncated_numbers(
        jax.nn.sigmoid(split_pre[:latent_tensor]) * split_pre[latent_tensor : 2 * latent_tensor]
    )
    target_masked = truncated_numbers(
        jax.nn.sigmoid(split_pre[2 * latent_tensor : 3 * latent_tensor])
        * split_pre[3 * latent_tensor :]
    )
    return (standardized_edges, gate_pre, split_pre, source_masked, target_masked)


def grouped(values, groups):
    return values.reshape((groups, values.shape[0] // groups) + values.shape[1:])


def gathered(values, axis):
    groups = lax.axis_size("dap")
    copies = jnp.broadcast_to(values[None], (groups,) + values.shape)
    return jnp.moveaxis(lax.all_to_all(copies, "dap", 0, 0, tiled=True), 0, axis)


def exchanged(values):
    return lax.all_to_all(values, "dap", split_axis=0, concat_axis=0, tiled=True)


def totalled(parts):
    groups = lax.axis_size("dap")
    flat = jnp.concatenate([part.reshape(-1) for part in parts])
    unit = groups * 16 * 128
    padded = -(-flat.size // unit) * unit
    blocks = jnp.pad(flat, (0, padded - flat.size)).reshape(groups, -1, 128)
    mine = exchanged(truncated_numbers(blocks)).astype(jnp.float32).sum(axis=0)
    whole = gathered(truncated_numbers(mine), 0).astype(jnp.float32).reshape(-1)
    out, place = ([], 0)
    for part in parts:
        out.append(whole[place : place + part.size].reshape(part.shape))
        place += part.size
    return out


def to_channels(*rows):
    groups = lax.axis_size("dap")
    packed = jnp.stack([grouped(values, groups) for values in rows], axis=1)
    received = exchanged(packed)
    return [
        jnp.moveaxis(received[:, at], 0, 1).reshape(received.shape[2], -1, received.shape[4])[None]
        for at in range(len(rows))
    ]


def to_rows(*columns):
    groups = lax.axis_size("dap")
    packed = jnp.stack(
        [
            jnp.moveaxis(values[0].reshape(values.shape[1], groups, -1, values.shape[3]), 1, 0)
            for values in columns
        ],
        axis=1,
    )
    received = exchanged(packed)
    return [received[:, at].reshape((-1,) + received.shape[3:]) for at in range(len(columns))]


def contract_items(left_cols, right_cols, outgoing):
    if outgoing:
        return jnp.einsum(
            "xqik,xqjk->xqij", left_cols, right_cols, preferred_element_type=jnp.float32
        )
    return jnp.einsum("xqki,xqkj->xqij", left_cols, right_cols, preferred_element_type=jnp.float32)


def contract_back_items(grad_cols, left_cols, right_cols, outgoing):
    if outgoing:
        source_adjoint = jnp.einsum(
            "xqij,xqjk->xqik", grad_cols, right_cols, preferred_element_type=jnp.float32
        )
        target_adjoint = jnp.einsum(
            "xqij,xqik->xqjk", grad_cols, left_cols, preferred_element_type=jnp.float32
        )
    else:
        source_adjoint = jnp.einsum(
            "xqij,xqkj->xqki", grad_cols, right_cols, preferred_element_type=jnp.float32
        )
        target_adjoint = jnp.einsum(
            "xqij,xqki->xqkj", grad_cols, left_cols, preferred_element_type=jnp.float32
        )
    return (truncated_numbers(source_adjoint), truncated_numbers(target_adjoint))


def triangle_forward(edge_entry, linear_mapping, final, outgoing):
    latent_tensor = final.shape[0]
    groups = lax.axis_size("dap")
    standardized_edges, gate_pre, split_pre, source_masked, target_masked = sigmoid_pieces(
        edge_entry, linear_mapping, latent_tensor
    )
    kept = to_channels(source_masked, target_masked)
    triangle_cols = truncated_numbers(contract_items(kept[0], kept[1], outgoing))
    (triangle,) = to_rows(triangle_cols)
    unit_norm = truncated_numbers(edge_standardized(triangle.astype(jnp.float32), 0))
    values = jnp.einsum("crn,cz->rnz", unit_norm, final, preferred_element_type=jnp.float32)
    pair_new = truncated_numbers(edge_entry.astype(jnp.float32) + jax.nn.sigmoid(gate_pre) * values)
    return (pair_new, triangle, kept)


def triangle_back(edge_entry, linear_mapping, final, outgoing, triangle, kept, gradient):
    latent_tensor = final.shape[0]
    groups = lax.axis_size("dap")
    standardized_edges, gate_pre, split_pre, source_masked, target_masked = sigmoid_pieces(
        edge_entry, linear_mapping, latent_tensor
    )
    sigmoid_factor = jax.nn.sigmoid(gate_pre)
    tri_wide = triangle.astype(jnp.float32)
    unit_norm = truncated_numbers(edge_standardized(tri_wide, 0))
    values = jnp.einsum("crn,cz->rnz", unit_norm, final, preferred_element_type=jnp.float32)
    scaled = truncated_numbers(gradient * sigmoid_factor)
    final_sum = jnp.einsum("crn,rnz->cz", unit_norm, scaled, preferred_element_type=jnp.float32)
    grad_unit = jnp.einsum("rnz,cz->crn", scaled, final, preferred_element_type=jnp.float32)
    adjoint_sigmoid = truncated_numbers(gradient * values * sigmoid_factor * (1.0 - sigmoid_factor))
    grad_triangle = truncated_numbers(standardizer_adjoint(tri_wide, grad_unit, 0))
    (gradient_cols,) = to_channels(grad_triangle)
    left_back, right_back = contract_back_items(gradient_cols, kept[0], kept[1], outgoing)
    source_adjoint, target_adjoint = [
        values.astype(jnp.float32) for values in to_rows(left_back, right_back)
    ]
    logistic_primary = jax.nn.sigmoid(split_pre[:latent_tensor])
    logistic_tertiary = jax.nn.sigmoid(split_pre[2 * latent_tensor : 3 * latent_tensor])
    grad_split = truncated_numbers(
        jnp.concatenate(
            [
                source_adjoint
                * split_pre[latent_tensor : 2 * latent_tensor]
                * logistic_primary
                * (1.0 - logistic_primary),
                source_adjoint * logistic_primary,
                target_adjoint
                * split_pre[3 * latent_tensor :]
                * logistic_tertiary
                * (1.0 - logistic_tertiary),
                target_adjoint * logistic_tertiary,
            ],
            axis=0,
        )
    )
    proj_sum = jnp.concatenate(
        [
            jnp.einsum(
                "rnz,crn->zc", standardized_edges, grad_split, preferred_element_type=jnp.float32
            ),
            jnp.einsum(
                "rnz,rnc->zc",
                standardized_edges,
                adjoint_sigmoid,
                preferred_element_type=jnp.float32,
            ),
        ],
        axis=1,
    )
    grad_norm = jnp.einsum(
        "crn,zc->rnz",
        grad_split,
        linear_mapping[:, : 4 * latent_tensor],
        preferred_element_type=jnp.float32,
    )
    grad_norm = grad_norm + jnp.dot(
        adjoint_sigmoid,
        linear_mapping[:, 4 * latent_tensor :].T,
        preferred_element_type=jnp.float32,
    )
    grad_pair = gradient + standardizer_adjoint(edge_entry.astype(jnp.float32), grad_norm, 2)
    return (grad_pair, proj_sum, final_sum)


def shards(
    edge_embedding,
    alignment_embedding,
    tensor_flank_matrix,
    tensor_final_matrix,
    outward_sigmoid_matrix,
    outward_final_matrix,
    inward_sigmoid_matrix,
    inward_final_matrix,
    adjoint_seed,
):
    rows_here = edge_embedding.shape[0]
    residues = edge_embedding.shape[1]
    alignment_depth = alignment_embedding.shape[0]
    contraction_extent = tensor_flank_matrix.shape[1] // 2
    alignment_standardized = truncated_numbers(
        edge_standardized(alignment_embedding.astype(jnp.float32), 2)
    )
    alignment_mapped = jnp.dot(
        alignment_standardized, tensor_flank_matrix, preferred_element_type=jnp.float32
    )
    tensor_source_factor = truncated_numbers(alignment_mapped[..., :contraction_extent])
    tensor_target_factor = truncated_numbers(alignment_mapped[..., contraction_extent:])
    right_all = gathered(tensor_target_factor, 1).reshape(
        alignment_depth, residues, contraction_extent
    )
    tile_lines = 128 if residues % 128 == 0 else residues
    tile_number = residues // tile_lines
    outer_parts = []
    first_parts = []
    for block_index in range(tile_number):
        lower = block_index * tile_lines
        right_block = right_all[:, lower : lower + tile_lines]
        triangle_contraction = jnp.einsum(
            "sic,sjd->ijcd", tensor_source_factor, right_block, preferred_element_type=jnp.float32
        )
        outer_block = truncated_numbers(
            triangle_contraction.reshape(
                rows_here, tile_lines, contraction_extent * contraction_extent
            )
            / alignment_depth
        )
        update = jnp.dot(outer_block, tensor_final_matrix, preferred_element_type=jnp.float32)
        first_parts.append(
            truncated_numbers(
                edge_embedding[:, lower : lower + tile_lines].astype(jnp.float32) + update
            )
        )
        outer_parts.append(outer_block)
    outer_mean = jnp.concatenate(outer_parts, axis=1)
    pair_one = jnp.concatenate(first_parts, axis=1)
    pair_two, triangle_out, kept_out = triangle_forward(
        pair_one, outward_sigmoid_matrix, outward_final_matrix, True
    )
    edge_embedding_updated, triangle_in, kept_in = triangle_forward(
        pair_two, inward_sigmoid_matrix, inward_final_matrix, False
    )
    grad_two, inward_sigmoid_accrual, inward_final_accrual = triangle_back(
        pair_two,
        inward_sigmoid_matrix,
        inward_final_matrix,
        False,
        triangle_in,
        kept_in,
        adjoint_seed.astype(jnp.float32),
    )
    grad_one, outward_sigmoid_accrual, outward_final_accrual = triangle_back(
        pair_one,
        outward_sigmoid_matrix,
        outward_final_matrix,
        True,
        triangle_out,
        kept_out,
        grad_two,
    )
    edge_embedding_adjoint = truncated_numbers(grad_one)
    tensor_final_accrual = jnp.einsum(
        "rnk,rnz->kz", outer_mean, edge_embedding_adjoint, preferred_element_type=jnp.float32
    )
    source_adjoint = jnp.zeros((alignment_depth, rows_here, contraction_extent), jnp.float32)
    outer_grads = []
    for block_index in range(tile_number):
        lower = block_index * tile_lines
        right_block = right_all[:, lower : lower + tile_lines]
        adjoint_tensor_mean = truncated_numbers(
            jnp.dot(
                edge_embedding_adjoint[:, lower : lower + tile_lines],
                tensor_final_matrix.T,
                preferred_element_type=jnp.float32,
            )
        )
        adjoint_tensor_mean = adjoint_tensor_mean.reshape(
            rows_here, tile_lines, contraction_extent, contraction_extent
        )
        source_adjoint = (
            source_adjoint
            + jnp.einsum(
                "mopz,loz->lmp",
                adjoint_tensor_mean,
                right_block,
                preferred_element_type=jnp.float32,
            )
            / alignment_depth
        )
        outer_grads.append(adjoint_tensor_mean)
    pair_columns = lax.all_to_all(
        edge_embedding_adjoint, "dap", split_axis=1, concat_axis=0, tiled=True
    )
    left_all = gathered(tensor_source_factor, 1).reshape(
        alignment_depth, residues, contraction_extent
    )
    target_adjoint = jnp.zeros((alignment_depth, rows_here, contraction_extent), jnp.float32)
    for block_index in range(tile_number):
        lower = block_index * tile_lines
        column_grad = truncated_numbers(
            jnp.dot(
                pair_columns[lower : lower + tile_lines],
                tensor_final_matrix.T,
                preferred_element_type=jnp.float32,
            )
        )
        column_grad = column_grad.reshape(
            tile_lines, rows_here, contraction_extent, contraction_extent
        )
        target_adjoint = (
            target_adjoint
            + jnp.einsum(
                "gxqp,vgq->vxp",
                column_grad,
                left_all[:, lower : lower + tile_lines],
                preferred_element_type=jnp.float32,
            )
            / alignment_depth
        )
    alignment_mapped_adjoint = truncated_numbers(
        jnp.concatenate([source_adjoint, target_adjoint], axis=2)
    )
    tensor_flank_accrual = jnp.einsum(
        "ajo,ajm->om",
        alignment_standardized,
        alignment_mapped_adjoint,
        preferred_element_type=jnp.float32,
    )
    alignment_standard_adjoint = jnp.dot(
        alignment_mapped_adjoint, tensor_flank_matrix.T, preferred_element_type=jnp.float32
    )
    alignment_adjoint = truncated_numbers(
        standardizer_adjoint(alignment_embedding.astype(jnp.float32), alignment_standard_adjoint, 2)
    )
    totals = totalled(
        (
            tensor_flank_accrual,
            tensor_final_accrual,
            outward_sigmoid_accrual,
            outward_final_accrual,
            inward_sigmoid_accrual,
            inward_final_accrual,
        )
    )
    return (
        edge_embedding_updated,
        edge_embedding_adjoint,
        alignment_adjoint,
        totals[0] / residues,
        totals[1] / residues,
        totals[2] / residues,
        totals[3] / residues,
        totals[4] / residues,
        totals[5] / residues,
    )


def solution(mesh):
    placed = (
        P(("dp", "dap"), None, None),
        P("dp", "dap", None),
        P(),
        P(),
        P(),
        P(),
        P(),
        P(),
        P(("dp", "dap"), None, None),
    )
    return jax.shard_map(
        shards,
        mesh=mesh,
        in_specs=placed,
        out_specs=(
            P(("dp", "dap"), None, None),
            P(("dp", "dap"), None, None),
            P("dp", "dap", None),
            P("dp", None),
            P("dp", None),
            P("dp", None),
            P("dp", None),
            P("dp", None),
            P("dp", None),
        ),
        check_vma=False,
    )
```

profile of v0, /device:TPU:0, one launch (start us, length us, event | category | flops | bytes accessed | tf_op | source)
XLA Modules:
  0.0 255.0 jit_solution(16639720308278416110)
XLA Ops:
  6.6 8.3 %all-to-all-start = ((bf16[16,2,6144]{2,1,0:T(2,128)(2,1)}), bf16[16,2,6144]{2,1,0:T(2,128)(2,1)S(1)}, u32[]{:S(2)}, u32[]{:S(2)}) async-start(bf16[16,2,6144]{2,1,0:T(2,128)(2,1)} %reshape.289), calls=%async_computation | async-start | bytes 786432 | tf_op jit(solution)/shard_map/all_to_all | solution.py:62
  14.9 12.6 %all-to-all-done = bf16[16,2,6144]{2,1,0:T(2,128)(2,1)S(1)} async-done(((bf16[16,2,6144]{2,1,0:T(2,128)(2,1)}), bf16[16,2,6144]{2,1,0:T(2,128)(2,1)S(1)}, u32[]{:S(2)}, u32[]{:S(2)}) %all-to-all-start) | async-done | bytes 393248 | tf_op jit(solution)/shard_map/all_to_all | solution.py:62
  32.4 15.4 %all_to_all.78 = bf16[16,2,8,6,96]{4,2,3,1,0:T(8,128)(2,1)S(1)} all-to-all(bf16[16,2,8,6,96]{4,2,3,1,0:T(8,128)(2,1)S(1)} %copy.175), channel_id=1, replica_groups=mesh['dap'=16,'dp'=2] {'dap'}, dimensions={0} | all-to-all | bytes 589824 | tf_op jit(solution)/shard_map/all_to_all | solution.py:66
  48.5 11.5 %all_to_all.79 = bf16[16,1,8,6,96]{4,2,3,1,0:T(8,128)(2,1)S(1)} all-to-all(bf16[16,1,8,6,96]{4,2,3,1,0:T(8,128)(2,1)S(1)} %bitcast.340), channel_id=1, replica_groups=mesh['dap'=16,'dp'=2] {'dap'}, dimensions={0} | all-to-all | bytes 294912 | tf_op jit(solution)/shard_map/all_to_all | solution.py:66
  61.5 1.8 fusion.74
  71.3 13.2 %all_to_all.80 = bf16[16,2,8,6,96]{4,2,3,1,0:T(8,128)(2,1)S(1)} all-to-all(bf16[16,2,8,6,96]{4,2,3,1,0:T(8,128)(2,1)S(1)} %copy.186), channel_id=1, replica_groups=mesh['dap'=16,'dp'=2] {'dap'}, dimensions={0} | all-to-all | bytes 589824 | tf_op jit(solution)/shard_map/all_to_all | solution.py:66
  85.3 11.8 %all_to_all.81 = bf16[16,1,8,6,96]{4,2,3,1,0:T(8,128)(2,1)S(1)} all-to-all(bf16[16,1,8,6,96]{4,2,3,1,0:T(8,128)(2,1)S(1)} %bitcast.341), channel_id=1, replica_groups=mesh['dap'=16,'dp'=2] {'dap'}, dimensions={0} | all-to-all | bytes 294912 | tf_op jit(solution)/shard_map/all_to_all | solution.py:66
  98.5 1.9 copy.194
  104.6 2.1 fusion.79
  111.1 11.1 %all_to_all.82 = bf16[16,1,8,6,96]{4,2,3,1,0:T(8,128)(2,1)S(1)} all-to-all(bf16[16,1,8,6,96]{4,2,3,1,0:T(8,128)(2,1)S(1)} %copy.196), channel_id=1, replica_groups=mesh['dap'=16,'dp'=2] {'dap'}, dimensions={0} | all-to-all | bytes 294912 | tf_op jit(solution)/shard_map/all_to_all | solution.py:66
  124.7 4.4 %all-to-all-start.6 = ((bf16[16,2,8,6,96]{4,2,3,1,0:T(8,128)(2,1)}), bf16[16,2,8,6,96]{4,2,3,1,0:T(8,128)(2,1)}, u32[]{:S(2)}, u32[]{:S(2)}) async-start(bf16[16,2,8,6,96]{4,2,3,1,0:T(8,128)(2,1)} %copy.203), calls=%async_computation.6 | async-start | bytes 786432 | tf_op jit(solution)/shard_map/all_to_all | solution.py:66
  129.1 1.8 broadcast_bitcast_fusion
  130.9 2.7 %reshape.291 = bf16[16,2,6144]{2,1,0:T(2,128)(2,1)} reshape(bf16[16,6,32,64]{3,2,1,0:T(8,128)(2,1)} %broadcast_bitcast_fusion) | data formatting | bytes 786432
  133.6 4.9 %all-to-all-done.6 = bf16[16,2,8,6,96]{4,2,3,1,0:T(8,128)(2,1)} async-done(((bf16[16,2,8,6,96]{4,2,3,1,0:T(8,128)(2,1)}), bf16[16,2,8,6,96]{4,2,3,1,0:T(8,128)(2,1)}, u32[]{:S(2)}, u32[]{:S(2)}) %all-to-all-start.6) | async-done | bytes 294944 | tf_op jit(solution)/shard_map/all_to_all | solution.py:66
  138.6 4.2 %all-to-all-start.9 = ((bf16[16,2,6144]{2,1,0:T(2,128)(2,1)}), bf16[16,2,6144]{2,1,0:T(2,128)(2,1)}, u32[]{:S(2)}, u32[]{:S(2)}) async-start(bf16[16,2,6144]{2,1,0:T(2,128)(2,1)} %reshape.291), calls=%async_computation.9 | async-start | bytes 786432 | tf_op jit(solution)/shard_map/all_to_all | solution.py:62
  142.8 1.8 slice_convert_fusion.3
  145.4 1.9 copy.205
  147.2 1.8 copy.295
  149.0 1.9 copy.208
  157.4 6.9 %all-to-all-start.7 = ((bf16[16,1,8,6,96]{4,2,3,1,0:T(8,128)(2,1)}), bf16[16,1,8,6,96]{4,2,3,1,0:T(8,128)(2,1)}, u32[]{:S(2)}, u32[]{:S(2)}) async-start(bf16[16,1,8,6,96]{4,2,3,1,0:T(8,128)(2,1)} %copy.211), calls=%async_computation.7 | async-start | bytes 393216 | tf_op jit(solution)/shard_map/all_to_all | solution.py:66
  164.3 2.7 %reshape.292 = bf16[16,6,32,64]{3,2,1,0:T(8,128)(2,1)} reshape(bf16[16,2,6144]{2,1,0:T(2,128)(2,1)} %all-to-all-done.9) | data formatting | bytes 786432
  167.0 2.7 %copy.232 = bf16[64,96,32]{1,0,2:T(8,128)(2,1)} copy(bf16[64,96,32]{0,2,1:T(8,128)(2,1)} %bitcast.322) | data formatting | bytes 786432 | tf_op jit(solution)/shard_map/reshape | solution.py:324
  176.0 6.7 %all-to-all-start.8 = ((bf16[16,2,8,6,96]{4,2,3,1,0:T(8,128)(2,1)}), bf16[16,2,8,6,96]{4,2,3,1,0:T(8,128)(2,1)S(1)}, u32[]{:S(2)}, u32[]{:S(2)}) async-start(bf16[16,2,8,6,96]{4,2,3,1,0:T(8,128)(2,1)} %copy.218), calls=%async_computation.8 | async-start | bytes 786432 | tf_op jit(solution)/shard_map/all_to_all | solution.py:66
  184.6 7.6 %all-to-all-done.8 = bf16[16,2,8,6,96]{4,2,3,1,0:T(8,128)(2,1)S(1)} async-done(((bf16[16,2,8,6,96]{4,2,3,1,0:T(8,128)(2,1)}), bf16[16,2,8,6,96]{4,2,3,1,0:T(8,128)(2,1)S(1)}, u32[]{:S(2)}, u32[]{:S(2)}) %all-to-all-start.8) | async-done | bytes 294944 | tf_op jit(solution)/shard_map/all_to_all | solution.py:66
  196.4 3.8 %all-to-all-start.10 = ((bf16[6,96,128]{2,0,1:T(8,128)(2,1)}), bf16[6,96,128]{2,0,1:T(8,128)(2,1)S(1)}, u32[]{:S(2)}, u32[]{:S(2)}) async-start(bf16[6,96,128]{2,0,1:T(8,128)(2,1)} %copy.228), calls=%async_computation.10 | async-start | bytes 393216 | tf_op jit(solution)/shard_map/all_to_all | solution.py:321
  202.6 2.6 %fusion.28 = bf16[64,6,32]{0,2,1:T(8,128)(2,1)} fusion(bf16[6,96,32,32]{1,3,2,0:T(8,128)(2,1)} %bitcast.338, bf16[64,96,32]{1,0,2:T(8,128)(2,1)S(1)} %copy-done.46), kind=kOutput, calls=%fused_computation.47 | convolution fusion | flops 75522048 | bytes 1597440 | tf_op jit(solution)/shard_map/mopz,loz->lmp/dot_general | solution.py:312
  205.3 3.0 %all-to-all-done.10 = bf16[6,96,128]{2,0,1:T(8,128)(2,1)S(1)} async-done(((bf16[6,96,128]{2,0,1:T(8,128)(2,1)}), bf16[6,96,128]{2,0,1:T(8,128)(2,1)S(1)}, u32[]{:S(2)}, u32[]{:S(2)}) %all-to-all-start.10) | async-done | bytes 147488 | tf_op jit(solution)/shard_map/all_to_all | solution.py:321
  209.8 1.7 fusion.31
  213.4 17.6 %all_to_all.83 = bf16[16,176,128]{2,1,0:T(8,128)(2,1)S(1)} all-to-all(bf16[16,176,128]{2,1,0:T(8,128)(2,1)S(1)} %bitcast.323), channel_id=1, replica_groups=mesh['dap'=16,'dp'=2] {'dap'}, dimensions={0} | all-to-all | bytes 1441792 | tf_op jit(solution)/shard_map/all_to_all | solution.py:66
  232.1 3.6 %all-to-all-start.12 = ((bf16[16,176,128]{2,1,0:T(8,128)(2,1)}), bf16[16,176,128]{2,1,0:T(8,128)(2,1)S(1)}, u32[]{:S(2)}, u32[]{:S(2)}) async-start(bf16[16,176,128]{2,1,0:T(8,128)(2,1)} %broadcast_in_dim.8), calls=%async_computation.12 | async-start | bytes 1441792 | tf_op jit(solution)/shard_map/all_to_all | solution.py:62
  237.1 11.2 %all-to-all-done.12 = bf16[16,176,128]{2,1,0:T(8,128)(2,1)S(1)} async-done(((bf16[16,176,128]{2,1,0:T(8,128)(2,1)}), bf16[16,176,128]{2,1,0:T(8,128)(2,1)S(1)}, u32[]{:S(2)}, u32[]{:S(2)}) %all-to-all-start.12) | async-done | bytes 720928 | tf_op jit(solution)/shard_map/all_to_all | solution.py:62
  249.9 1.8 slice.132
  (290 shorter events, 65.7 us)
Async XLA Ops:
  0.6 29.3 %copy-start = (bf16[1024,128]{1,0:T(8,128)(2,1)S(1)}, bf16[1024,128]{1,0:T(8,128)(2,1)}, u32[]{:S(2)}) copy-start(bf16[1024,128]{1,0:T(8,128)(2,1)} %param.12) | copy-start | bytes 786436
  1.8 3.3 %copy-start.56 = (f32[64,6]{0,1:T(8,128)}, f32[64,6]{0,1:T(8,128)S(1)}, u32[]{:S(2)}) copy-start(f32[64,6]{0,1:T(8,128)S(1)} %broadcast_multiply_fusion.14) | copy-start | bytes 4612
  5.1 22.9 %copy-start.47 = (bf16[64,6,32]{0,2,1:T(8,128)(2,1)}, bf16[64,6,32]{0,2,1:T(8,128)(2,1)S(1)}, u32[]{:S(2)}) copy-start(bf16[64,6,32]{0,2,1:T(8,128)(2,1)S(1)} %get-tuple-element.79) | copy-start | bytes 73732
  6.6 21.0 %all-to-all-start = ((bf16[16,2,6144]{2,1,0:T(2,128)(2,1)}), bf16[16,2,6144]{2,1,0:T(2,128)(2,1)S(1)}, u32[]{:S(2)}, u32[]{:S(2)}) async-start(bf16[16,2,6144]{2,1,0:T(2,128)(2,1)} %reshape.289), calls=%async_computation | async-start | bytes 786432 | tf_op jit(solution)/shard_map/all_to_all | solution.py:62
  31.3 30.2 %copy-start.12 = (bf16[6,96,128]{2,1,0:T(8,128)(2,1)}, bf16[6,96,128]{2,1,0:T(8,128)(2,1)S(1)}, u32[]{:S(2)}) copy-start(bf16[6,96,128]{2,1,0:T(8,128)(2,1)S(1)} %fusion.58) | copy-start | bytes 442372
  47.9 12.2 %copy-start.18 = (bf16[16,1,8,6,96]{4,2,3,1,0:T(8,128)(2,1)}, bf16[16,1,8,6,96]{4,2,3,1,0:T(8,128)(2,1)S(1)}, u32[]{:S(2)}) copy-start(bf16[16,1,8,6,96]{4,2,3,1,0:T(8,128)(2,1)S(1)} %get-tuple-element.78) | copy-start | bytes 442372
  48.1 13.2 %copy-start.54 = (bf16[128,128]{1,0:T(8,128)(2,1)S(1)}, bf16[128,128]{1,0:T(8,128)(2,1)}, u32[]{:S(2)}) copy-start(bf16[128,128]{1,0:T(8,128)(2,1)} %param.14) | copy-start | bytes 98308
  60.2 3.0 %copy-start.4 = (f32[128,6,96]{0,2,1:T(8,128)}, f32[128,6,96]{0,2,1:T(8,128)S(1)}, u32[]{:S(2)}) copy-start(f32[128,6,96]{0,2,1:T(8,128)S(1)} %copy.183) | copy-start | bytes 884740
  60.3 3.4 %copy-start.60 = (f32[6,96]{1,0:T(8,128)}, f32[6,96]{1,0:T(8,128)S(1)}, u32[]{:S(2)}) copy-start(f32[6,96]{1,0:T(8,128)S(1)} %broadcast_multiply_fusion.10) | copy-start | bytes 6916
  60.4 3.3 %copy-start.68 = (f32[6,96]{1,0:T(8,128)}, f32[6,96]{1,0:T(8,128)S(1)}, u32[]{:S(2)}) copy-start(f32[6,96]{1,0:T(8,128)S(1)} %add_rsqrt_fusion.2) | copy-start | bytes 6916
  61.3 4.2 %copy-start.42 = (bf16[128,640]{1,0:T(8,128)(2,1)S(1)}, bf16[128,640]{1,0:T(8,128)(2,1)}, u32[]{:S(2)}) copy-start(bf16[128,640]{1,0:T(8,128)(2,1)} %param.15) | copy-start | bytes 491524
  102.3 4.3 %copy-start.6 = (f32[128,6,96]{0,2,1:T(8,128)S(1)}, f32[128,6,96]{0,2,1:T(8,128)}, u32[]{:S(2)}) copy-start(f32[128,6,96]{0,2,1:T(8,128)} %copy.194) | copy-start | bytes 884740
  102.4 4.3 %copy-start.53 = (bf16[128,128]{1,0:T(8,128)(2,1)S(1)}, bf16[128,128]{1,0:T(8,128)(2,1)}, u32[]{:S(2)}) copy-start(bf16[128,128]{1,0:T(8,128)(2,1)} %param.16) | copy-start | bytes 98308
  103.6 3.6 %copy-start.29 = (bf16[128,6,96]{0,2,1:T(8,128)(2,1)}, bf16[128,6,96]{0,2,1:T(8,128)(2,1)S(1)}, u32[]{:S(2)}) copy-start(bf16[128,6,96]{0,2,1:T(8,128)(2,1)S(1)} %fusion.96) | copy-start | bytes 442372
  110.1 13.3 %copy-start.22 = (bf16[16,1,8,6,96]{4,2,3,1,0:T(8,128)(2,1)S(1)}, bf16[16,1,8,6,96]{4,2,3,1,0:T(8,128)(2,1)}, u32[]{:S(2)}) copy-start(bf16[16,1,8,6,96]{4,2,3,1,0:T(8,128)(2,1)} %copy-done.21) | copy-start | bytes 442372
  124.7 13.9 %all-to-all-start.6 = ((bf16[16,2,8,6,96]{4,2,3,1,0:T(8,128)(2,1)}), bf16[16,2,8,6,96]{4,2,3,1,0:T(8,128)(2,1)}, u32[]{:S(2)}, u32[]{:S(2)}) async-start(bf16[16,2,8,6,96]{4,2,3,1,0:T(8,128)(2,1)} %copy.203), calls=%async_computation.6 | async-start | bytes 786432 | tf_op jit(solution)/shard_map/all_to_all | solution.py:66
  138.6 18.8 %all-to-all-start.9 = ((bf16[16,2,6144]{2,1,0:T(2,128)(2,1)}), bf16[16,2,6144]{2,1,0:T(2,128)(2,1)}, u32[]{:S(2)}, u32[]{:S(2)}) async-start(bf16[16,2,6144]{2,1,0:T(2,128)(2,1)} %reshape.291), calls=%async_computation.9 | async-start | bytes 786432 | tf_op jit(solution)/shard_map/all_to_all | solution.py:62
  155.6 11.4 %copy-start.31 = (bf16[6,96,128]{2,1,0:T(8,128)(2,1)}, bf16[6,96,128]{2,1,0:T(8,128)(2,1)S(1)}, u32[]{:S(2)}) copy-start(bf16[6,96,128]{2,1,0:T(8,128)(2,1)S(1)} %multiply_convert_fusion.7) | copy-start | bytes 442372
  157.4 15.0 %all-to-all-start.7 = ((bf16[16,1,8,6,96]{4,2,3,1,0:T(8,128)(2,1)}), bf16[16,1,8,6,96]{4,2,3,1,0:T(8,128)(2,1)}, u32[]{:S(2)}, u32[]{:S(2)}) async-start(bf16[16,1,8,6,96]{4,2,3,1,0:T(8,128)(2,1)} %copy.211), calls=%async_computation.7 | async-start | bytes 393216 | tf_op jit(solution)/shard_map/all_to_all | solution.py:66
  167.0 4.4 %copy-start.15 = (bf16[6,96,128]{2,1,0:T(8,128)(2,1)S(1)}, bf16[6,96,128]{2,1,0:T(8,128)(2,1)}, u32[]{:S(2)}) copy-start(bf16[6,96,128]{2,1,0:T(8,128)(2,1)} %copy-done.14) | copy-start | bytes 442372
  167.0 4.4 %copy-start.39 = (bf16[6,96,128]{2,1,0:T(8,128)(2,1)S(1)}, bf16[6,96,128]{2,1,0:T(8,128)(2,1)}, u32[]{:S(2)}) copy-start(bf16[6,96,128]{2,1,0:T(8,128)(2,1)} %get-tuple-element.68) | copy-start | bytes 442372
  169.7 4.9 %copy-start.19 = (bf16[16,1,8,6,96]{4,2,3,1,0:T(8,128)(2,1)S(1)}, bf16[16,1,8,6,96]{4,2,3,1,0:T(8,128)(2,1)}, u32[]{:S(2)}) copy-start(bf16[16,1,8,6,96]{4,2,3,1,0:T(8,128)(2,1)} %copy-done.18) | copy-start | bytes 442372
  175.1 7.9 %copy-start.52 = (bf16[128,128]{1,0:T(8,128)(2,1)S(1)}, bf16[128,128]{1,0:T(8,128)(2,1)}, u32[]{:S(2)}) copy-start(bf16[128,128]{1,0:T(8,128)(2,1)} %fusion.36) | copy-start | bytes 98308
  175.2 8.6 %copy-start.13 = (bf16[6,96,128]{2,1,0:T(8,128)(2,1)S(1)}, bf16[6,96,128]{2,1,0:T(8,128)(2,1)}, u32[]{:S(2)}) copy-start(bf16[6,96,128]{2,1,0:T(8,128)(2,1)} %copy-done.12) | copy-start | bytes 442372
  175.2 8.6 %copy-start.24 = (bf16[6,96,128]{2,1,0:T(8,128)(2,1)S(1)}, bf16[6,96,128]{2,1,0:T(8,128)(2,1)}, u32[]{:S(2)}) copy-start(bf16[6,96,128]{2,1,0:T(8,128)(2,1)} %get-tuple-element.46) | copy-start | bytes 442372
  176.0 16.3 %all-to-all-start.8 = ((bf16[16,2,8,6,96]{4,2,3,1,0:T(8,128)(2,1)}), bf16[16,2,8,6,96]{4,2,3,1,0:T(8,128)(2,1)S(1)}, u32[]{:S(2)}, u32[]{:S(2)}) async-start(bf16[16,2,8,6,96]{4,2,3,1,0:T(8,128)(2,1)} %copy.218), calls=%async_computation.8 | async-start | bytes 786432 | tf_op jit(solution)/shard_map/all_to_all | solution.py:66
  196.4 11.9 %all-to-all-start.10 = ((bf16[6,96,128]{2,0,1:T(8,128)(2,1)}), bf16[6,96,128]{2,0,1:T(8,128)(2,1)S(1)}, u32[]{:S(2)}, u32[]{:S(2)}) async-start(bf16[6,96,128]{2,0,1:T(8,128)(2,1)} %copy.228), calls=%async_computation.10 | async-start | bytes 393216 | tf_op jit(solution)/shard_map/all_to_all | solution.py:321
  231.0 4.7 %copy-start.3 = (bf16[64,6,256]{2,0,1:T(8,128)(2,1)S(1)}, bf16[64,6,256]{2,0,1:T(8,128)(2,1)}, u32[]{:S(2)}) copy-start(bf16[64,6,256]{2,0,1:T(8,128)(2,1)} %param.10) | copy-start | bytes 589828
  231.0 4.7 %copy-start.50 = (bf16[256,64]{0,1:T(8,128)(2,1)S(1)}, bf16[256,64]{0,1:T(8,128)(2,1)}, u32[]{:S(2)}) copy-start(bf16[256,64]{0,1:T(8,128)(2,1)} %param.11) | copy-start | bytes 98308
  231.0 4.7 %copy-start.57 = (f32[64,6]{0,1:T(8,128)S(1)}, f32[64,6]{0,1:T(8,128)}, u32[]{:S(2)}) copy-start(f32[64,6]{0,1:T(8,128)} %copy-done.56) | copy-start | bytes 4612
  231.0 4.7 %copy-start.65 = (f32[64,6]{0,1:T(8,128)S(1)}, f32[64,6]{0,1:T(8,128)}, u32[]{:S(2)}) copy-start(f32[64,6]{0,1:T(8,128)} %copy-done.64) | copy-start | bytes 4612
  232.1 16.2 %all-to-all-start.12 = ((bf16[16,176,128]{2,1,0:T(8,128)(2,1)}), bf16[16,176,128]{2,1,0:T(8,128)(2,1)S(1)}, u32[]{:S(2)}, u32[]{:S(2)}) async-start(bf16[16,176,128]{2,1,0:T(8,128)(2,1)} %broadcast_in_dim.8), calls=%async_computation.12 | async-start | bytes 1441792 | tf_op jit(solution)/shard_map/all_to_all | solution.py:62
  (48 other events, 62.1 us)
where the time goes:
time: 257 us; the launch traced here: 255 us
  blocking collectives  80.6 us (31%)
  local copies, waits for them, and re-layouts  50.1 us (19%)
  waiting for transfers between devices  39.7 us (15%)
  starting transfers between devices  37.9 us (15%)
  matrix products  22.9 us (9%)
  other arithmetic  21.7 us (8%)
    all_to_all x6, blocking collectives, exchanged(): lax.all_to_all(values, 'dap', split_axis=0, concat_axis=0, tiled=True)  80.6 us
    all_to_all x3, waiting for transfers between devices, gathered(): lax.all_to_all(copies, 'dap', 0, 0, tiled=True)  23.9 us
    all_to_all x3, starting transfers between devices, exchanged(): lax.all_to_all(values, 'dap', split_axis=0, concat_axis=0, tiled=True)  17.9 us
    all_to_all x3, starting transfers between devices, gathered(): lax.all_to_all(copies, 'dap', 0, 0, tiled=True)  16.2 us
    unnamed x156, local copies, waits for them, and re-layouts  15.8 us
    all_to_all x3, waiting for transfers between devices, exchanged(): lax.all_to_all(values, 'dap', split_axis=0, concat_axis=0, tiled=True)  12.8 us
    optimization_barrier x15, local copies, waits for them, and re-layouts, truncated_numbers(): return lax.optimization_barrier(values.astype(jnp.bfloat16))  9.37 us
    convert_element_type x13, other arithmetic, truncated_numbers(): return lax.optimization_barrier(values.astype(jnp.bfloat16))  7.83 us
  transfers between devices with their start and end apart: 7, of which 6 were waited for; matrix products, arithmetic and copies ran while one was open for 13% of the time, Pallas kernels for 0%

commit v1 on v0

--- a/solution.py
+++ b/solution.py
@@ -1,9 +1,26 @@
+import functools
 import jax
 import jax.numpy as jnp
 from jax import lax
 from jax.sharding import PartitionSpec as P
 
 EPSILON = 1e-05
+
+
+def launch_slabs(field_in, across, where_dim, along_dim):
+    all_values = jnp.concatenate(
+        lax.all_to_all(
+            jnp.stack(jnp.split(field_in, lax.psum(1, across), axis=where_dim), axis=0),
+            across,
+            split_axis=0,
+            concat_axis=0,
+        ),
+        axis=along_dim,
+    )
+    return all_values
+
+
+indices_begin = functools.partial(launch_slabs, across="dap", where_dim=1, along_dim=0)
 
 
 def truncated_numbers(values):
@@ -318,9 +335,7 @@
             / alignment_depth
         )
         outer_grads.append(adjoint_tensor_mean)
-    pair_columns = lax.all_to_all(
-        edge_embedding_adjoint, "dap", split_axis=1, concat_axis=0, tiled=True
-    )
+    pair_columns = indices_begin(edge_embedding_adjoint)
     left_all = gathered(tensor_source_factor, 1).reshape(
         alignment_depth, residues, contraction_extent
     )

time: 257 us -> 266 us (1.035)
  local copies, waits for them, and re-layouts: 50.1 us -> 59 us
    unnamed x156 -> x171, local copies, waits for them, and re-layouts: 15.8 us -> 25 us
    optimization_barrier x15 -> x14, local copies, waits for them, and re-layouts: 9.37 us -> 8.62 us  [truncated_numbers(): return lax.optimization_barrier(values.astype(jnp.bfloat16))]
where the time goes in v1:
time: 266 us; the launch traced here: 264 us
  blocking collectives  80.6 us (30%)
  local copies, waits for them, and re-layouts  59 us (22%)
  waiting for transfers between devices  39.7 us (15%)
  starting transfers between devices  37.9 us (14%)
  matrix products  22.9 us (9%)
  other arithmetic  21.7 us (8%)
    all_to_all x6, blocking collectives, exchanged(): lax.all_to_all(values, 'dap', split_axis=0, concat_axis=0, tiled=True)  80.6 us
    unnamed x171, local copies, waits for them, and re-layouts  25 us
    all_to_all x3, waiting for transfers between devices, gathered(): lax.all_to_all(copies, 'dap', 0, 0, tiled=True)  23.9 us
    all_to_all x3, starting transfers between devices, exchanged(): lax.all_to_all(values, 'dap', split_axis=0, concat_axis=0, tiled=True)  17.9 us
    all_to_all x3, starting transfers between devices, gathered(): lax.all_to_all(copies, 'dap', 0, 0, tiled=True)  16.2 us
    all_to_all x3, waiting for transfers between devices, exchanged(): lax.all_to_all(values, 'dap', split_axis=0, concat_axis=0, tiled=True)  12.8 us
    optimization_barrier x14, local copies, waits for them, and re-layouts, truncated_numbers(): return lax.optimization_barrier(values.astype(jnp.bfloat16))  8.62 us
    convert_element_type x13, other arithmetic, truncated_numbers(): return lax.optimization_barrier(values.astype(jnp.bfloat16))  7.83 us
  transfers between devices with their start and end apart: 7, of which 6 were waited for; matrix products, arithmetic and copies ran while one was open for 13% of the time, Pallas kernels for 0%

profile of v1, /device:TPU:0, one launch (start us, length us, event | category | flops | bytes accessed | tf_op | source)
XLA Modules:
  0.0 263.9 jit_solution(870402508152713311)
XLA Ops:
  6.6 8.3 %all-to-all-start = ((bf16[16,2,6144]{2,1,0:T(2,128)(2,1)}), bf16[16,2,6144]{2,1,0:T(2,128)(2,1)S(1)}, u32[]{:S(2)}, u32[]{:S(2)}) async-start(bf16[16,2,6144]{2,1,0:T(2,128)(2,1)} %reshape.293), calls=%async_computation | async-start | bytes 786432 | tf_op jit(solution)/shard_map/all_to_all | solution.py:79
  14.9 12.6 %all-to-all-done = bf16[16,2,6144]{2,1,0:T(2,128)(2,1)S(1)} async-done(((bf16[16,2,6144]{2,1,0:T(2,128)(2,1)}), bf16[16,2,6144]{2,1,0:T(2,128)(2,1)S(1)}, u32[]{:S(2)}, u32[]{:S(2)}) %all-to-all-start) | async-done | bytes 393248 | tf_op jit(solution)/shard_map/all_to_all | solution.py:79
  32.4 15.4 %all_to_all.65 = bf16[16,2,8,6,96]{4,2,3,1,0:T(8,128)(2,1)S(1)} all-to-all(bf16[16,2,8,6,96]{4,2,3,1,0:T(8,128)(2,1)S(1)} %copy.173), channel_id=1, replica_groups=mesh['dap'=16,'dp'=2] {'dap'}, dimensions={0} | all-to-all | bytes 589824 | tf_op jit(solution)/shard_map/all_to_all | solution.py:83
  48.5 11.5 %all_to_all.66 = bf16[16,1,8,6,96]{4,2,3,1,0:T(8,128)(2,1)S(1)} all-to-all(bf16[16,1,8,6,96]{4,2,3,1,0:T(8,128)(2,1)S(1)} %bitcast.397), channel_id=1, replica_groups=mesh['dap'=16,'dp'=2] {'dap'}, dimensions={0} | all-to-all | bytes 294912 | tf_op jit(solution)/shard_map/all_to_all | solution.py:83
  61.5 1.8 fusion.74
  71.3 13.2 %all_to_all.67 = bf16[16,2,8,6,96]{4,2,3,1,0:T(8,128)(2,1)S(1)} all-to-all(bf16[16,2,8,6,96]{4,2,3,1,0:T(8,128)(2,1)S(1)} %copy.184), channel_id=1, replica_groups=mesh['dap'=16,'dp'=2] {'dap'}, dimensions={0} | all-to-all | bytes 589824 | tf_op jit(solution)/shard_map/all_to_all | solution.py:83
  85.3 11.8 %all_to_all.68 = bf16[16,1,8,6,96]{4,2,3,1,0:T(8,128)(2,1)S(1)} all-to-all(bf16[16,1,8,6,96]{4,2,3,1,0:T(8,128)(2,1)S(1)} %bitcast.398), channel_id=1, replica_groups=mesh['dap'=16,'dp'=2] {'dap'}, dimensions={0} | all-to-all | bytes 294912 | tf_op jit(solution)/shard_map/all_to_all | solution.py:83
  98.5 1.9 copy.192
  104.6 2.1 fusion.79
  111.1 11.1 %all_to_all.69 = bf16[16,1,8,6,96]{4,2,3,1,0:T(8,128)(2,1)S(1)} all-to-all(bf16[16,1,8,6,96]{4,2,3,1,0:T(8,128)(2,1)S(1)} %copy.194), channel_id=1, replica_groups=mesh['dap'=16,'dp'=2] {'dap'}, dimensions={0} | all-to-all | bytes 294912 | tf_op jit(solution)/shard_map/all_to_all | solution.py:83
  124.7 4.4 %all-to-all-start.6 = ((bf16[16,2,8,6,96]{4,2,3,1,0:T(8,128)(2,1)}), bf16[16,2,8,6,96]{4,2,3,1,0:T(8,128)(2,1)}, u32[]{:S(2)}, u32[]{:S(2)}) async-start(bf16[16,2,8,6,96]{4,2,3,1,0:T(8,128)(2,1)} %copy.201), calls=%async_computation.6 | async-start | bytes 786432 | tf_op jit(solution)/shard_map/all_to_all | solution.py:83
  129.1 1.8 broadcast_bitcast_fusion
  130.9 2.7 %reshape.295 = bf16[16,2,6144]{2,1,0:T(2,128)(2,1)} reshape(bf16[16,6,32,64]{3,2,1,0:T(8,128)(2,1)} %broadcast_bitcast_fusion) | data formatting | bytes 786432
  133.6 4.9 %all-to-all-done.6 = bf16[16,2,8,6,96]{4,2,3,1,0:T(8,128)(2,1)} async-done(((bf16[16,2,8,6,96]{4,2,3,1,0:T(8,128)(2,1)}), bf16[16,2,8,6,96]{4,2,3,1,0:T(8,128)(2,1)}, u32[]{:S(2)}, u32[]{:S(2)}) %all-to-all-start.6) | async-done | bytes 294944 | tf_op jit(solution)/shard_map/all_to_all | solution.py:83
  138.6 4.2 %all-to-all-start.9 = ((bf16[16,2,6144]{2,1,0:T(2,128)(2,1)}), bf16[16,2,6144]{2,1,0:T(2,128)(2,1)}, u32[]{:S(2)}, u32[]{:S(2)}) async-start(bf16[16,2,6144]{2,1,0:T(2,128)(2,1)} %reshape.295), calls=%async_computation.9 | async-start | bytes 786432 | tf_op jit(solution)/shard_map/all_to_all | solution.py:79
  142.8 1.8 slice_convert_fusion.3
  145.4 1.9 copy.203
  147.2 1.8 copy.291
  149.0 1.9 copy.206
  157.4 6.9 %all-to-all-start.7 = ((bf16[16,1,8,6,96]{4,2,3,1,0:T(8,128)(2,1)}), bf16[16,1,8,6,96]{4,2,3,1,0:T(8,128)(2,1)}, u32[]{:S(2)}, u32[]{:S(2)}) async-start(bf16[16,1,8,6,96]{4,2,3,1,0:T(8,128)(2,1)} %copy.209), calls=%async_computation.7 | async-start | bytes 393216 | tf_op jit(solution)/shard_map/all_to_all | solution.py:83
  164.3 2.7 %reshape.296 = bf16[16,6,32,64]{3,2,1,0:T(8,128)(2,1)} reshape(bf16[16,2,6144]{2,1,0:T(2,128)(2,1)} %all-to-all-done.9) | data formatting | bytes 786432
  167.0 2.7 %copy.228 = bf16[64,96,32]{1,0,2:T(8,128)(2,1)} copy(bf16[64,96,32]{0,2,1:T(8,128)(2,1)} %bitcast.380) | data formatting | bytes 786432 | tf_op jit(solution)/shard_map/reshape | solution.py:339
  176.0 6.7 %all-to-all-start.8 = ((bf16[16,2,8,6,96]{4,2,3,1,0:T(8,128)(2,1)}), bf16[16,2,8,6,96]{4,2,3,1,0:T(8,128)(2,1)S(1)}, u32[]{:S(2)}, u32[]{:S(2)}) async-start(bf16[16,2,8,6,96]{4,2,3,1,0:T(8,128)(2,1)} %copy.216), calls=%async_computation.8 | async-start | bytes 786432 | tf_op jit(solution)/shard_map/all_to_all | solution.py:83
  184.6 7.6 %all-to-all-done.8 = bf16[16,2,8,6,96]{4,2,3,1,0:T(8,128)(2,1)S(1)} async-done(((bf16[16,2,8,6,96]{4,2,3,1,0:T(8,128)(2,1)}), bf16[16,2,8,6,96]{4,2,3,1,0:T(8,128)(2,1)S(1)}, u32[]{:S(2)}, u32[]{:S(2)}) %all-to-all-start.8) | async-done | bytes 294944 | tf_op jit(solution)/shard_map/all_to_all | solution.py:83
  205.4 3.8 %all-to-all-start.10 = ((bf16[16,6,6,128]{3,2,1,0:T(8,128)(2,1)}), bf16[16,6,6,128]{3,2,1,0:T(8,128)(2,1)S(1)}, u32[]{:S(2)}, u32[]{:S(2)}) async-start(bf16[16,6,6,128]{3,2,1,0:T(8,128)(2,1)} %constant_dynamic-update-slice_fusion), calls=%async_computation.10 | async-start | bytes 393216 | tf_op jit(solution)/shard_map/all_to_all | solution.py:12
  211.6 2.6 fusion.28
  214.2 3.0 %all-to-all-done.10 = bf16[16,6,6,128]{3,2,1,0:T(8,128)(2,1)S(1)} async-done(((bf16[16,6,6,128]{3,2,1,0:T(8,128)(2,1)}), bf16[16,6,6,128]{3,2,1,0:T(8,128)(2,1)S(1)}, u32[]{:S(2)}, u32[]{:S(2)}) %all-to-all-start.10) | async-done | bytes 147488 | tf_op jit(solution)/shard_map/all_to_all | solution.py:12
  218.7 1.7 fusion.31
  222.3 17.6 %all_to_all.70 = bf16[16,176,128]{2,1,0:T(8,128)(2,1)S(1)} all-to-all(bf16[16,176,128]{2,1,0:T(8,128)(2,1)S(1)} %bitcast.381), channel_id=1, replica_groups=mesh['dap'=16,'dp'=2] {'dap'}, dimensions={0} | all-to-all | bytes 1441792 | tf_op jit(solution)/shard_map/all_to_all | solution.py:83
  240.9 3.6 %all-to-all-start.12 = ((bf16[16,176,128]{2,1,0:T(8,128)(2,1)}), bf16[16,176,128]{2,1,0:T(8,128)(2,1)S(1)}, u32[]{:S(2)}, u32[]{:S(2)}) async-start(bf16[16,176,128]{2,1,0:T(8,128)(2,1)} %broadcast_in_dim.8), calls=%async_computation.12 | async-start | bytes 1441792 | tf_op jit(solution)/shard_map/all_to_all | solution.py:79
  246.0 11.2 %all-to-all-done.12 = bf16[16,176,128]{2,1,0:T(8,128)(2,1)S(1)} async-done(((bf16[16,176,128]{2,1,0:T(8,128)(2,1)}), bf16[16,176,128]{2,1,0:T(8,128)(2,1)S(1)}, u32[]{:S(2)}, u32[]{:S(2)}) %all-to-all-start.12) | async-done | bytes 720928 | tf_op jit(solution)/shard_map/all_to_all | solution.py:79
  258.8 1.8 slice.132
  (303 shorter events, 74.6 us)
Async XLA Ops:
  0.6 29.3 %copy-start = (bf16[1024,128]{1,0:T(8,128)(2,1)S(1)}, bf16[1024,128]{1,0:T(8,128)(2,1)}, u32[]{:S(2)}) copy-start(bf16[1024,128]{1,0:T(8,128)(2,1)} %param.12) | copy-start | bytes 786436
  1.8 3.3 %copy-start.56 = (f32[64,6]{0,1:T(8,128)}, f32[64,6]{0,1:T(8,128)S(1)}, u32[]{:S(2)}) copy-start(f32[64,6]{0,1:T(8,128)S(1)} %broadcast_multiply_fusion.14) | copy-start | bytes 4612
  5.1 22.9 %copy-start.47 = (bf16[64,6,32]{0,2,1:T(8,128)(2,1)}, bf16[64,6,32]{0,2,1:T(8,128)(2,1)S(1)}, u32[]{:S(2)}) copy-start(bf16[64,6,32]{0,2,1:T(8,128)(2,1)S(1)} %get-tuple-element.79) | copy-start | bytes 73732
  6.6 21.0 %all-to-all-start = ((bf16[16,2,6144]{2,1,0:T(2,128)(2,1)}), bf16[16,2,6144]{2,1,0:T(2,128)(2,1)S(1)}, u32[]{:S(2)}, u32[]{:S(2)}) async-start(bf16[16,2,6144]{2,1,0:T(2,128)(2,1)} %reshape.293), calls=%async_computation | async-start | bytes 786432 | tf_op jit(solution)/shard_map/all_to_all | solution.py:79
  31.3 30.2 %copy-start.12 = (bf16[6,96,128]{2,1,0:T(8,128)(2,1)}, bf16[6,96,128]{2,1,0:T(8,128)(2,1)S(1)}, u32[]{:S(2)}) copy-start(bf16[6,96,128]{2,1,0:T(8,128)(2,1)S(1)} %fusion.58) | copy-start | bytes 442372
  47.9 12.2 %copy-start.18 = (bf16[16,1,8,6,96]{4,2,3,1,0:T(8,128)(2,1)}, bf16[16,1,8,6,96]{4,2,3,1,0:T(8,128)(2,1)S(1)}, u32[]{:S(2)}) copy-start(bf16[16,1,8,6,96]{4,2,3,1,0:T(8,128)(2,1)S(1)} %get-tuple-element.78) | copy-start | bytes 442372
  48.1 13.2 %copy-start.54 = (bf16[128,128]{1,0:T(8,128)(2,1)S(1)}, bf16[128,128]{1,0:T(8,128)(2,1)}, u32[]{:S(2)}) copy-start(bf16[128,128]{1,0:T(8,128)(2,1)} %param.14) | copy-start | bytes 98308
  60.3 3.4 %copy-start.60 = (f32[6,96]{1,0:T(8,128)}, f32[6,96]{1,0:T(8,128)S(1)}, u32[]{:S(2)}) copy-start(f32[6,96]{1,0:T(8,128)S(1)} %broadcast_multiply_fusion.10) | copy-start | bytes 6916
  60.4 3.3 %copy-start.68 = (f32[6,96]{1,0:T(8,128)}, f32[6,96]{1,0:T(8,128)S(1)}, u32[]{:S(2)}) copy-start(f32[6,96]{1,0:T(8,128)S(1)} %add_rsqrt_fusion.2) | copy-start | bytes 6916
  61.3 4.2 %copy-start.42 = (bf16[128,640]{1,0:T(8,128)(2,1)S(1)}, bf16[128,640]{1,0:T(8,128)(2,1)}, u32[]{:S(2)}) copy-start(bf16[128,640]{1,0:T(8,128)(2,1)} %param.15) | copy-start | bytes 491524
  102.3 4.3 %copy-start.6 = (f32[128,6,96]{0,2,1:T(8,128)S(1)}, f32[128,6,96]{0,2,1:T(8,128)}, u32[]{:S(2)}) copy-start(f32[128,6,96]{0,2,1:T(8,128)} %copy.192) | copy-start | bytes 884740
  102.4 4.3 %copy-start.53 = (bf16[128,128]{1,0:T(8,128)(2,1)S(1)}, bf16[128,128]{1,0:T(8,128)(2,1)}, u32[]{:S(2)}) copy-start(bf16[128,128]{1,0:T(8,128)(2,1)} %param.16) | copy-start | bytes 98308
  103.6 3.6 %copy-start.29 = (bf16[128,6,96]{0,2,1:T(8,128)(2,1)}, bf16[128,6,96]{0,2,1:T(8,128)(2,1)S(1)}, u32[]{:S(2)}) copy-start(bf16[128,6,96]{0,2,1:T(8,128)(2,1)S(1)} %fusion.96) | copy-start | bytes 442372
  110.1 13.3 %copy-start.22 = (bf16[16,1,8,6,96]{4,2,3,1,0:T(8,128)(2,1)S(1)}, bf16[16,1,8,6,96]{4,2,3,1,0:T(8,128)(2,1)}, u32[]{:S(2)}) copy-start(bf16[16,1,8,6,96]{4,2,3,1,0:T(8,128)(2,1)} %copy-done.21) | copy-start | bytes 442372
  124.7 13.9 %all-to-all-start.6 = ((bf16[16,2,8,6,96]{4,2,3,1,0:T(8,128)(2,1)}), bf16[16,2,8,6,96]{4,2,3,1,0:T(8,128)(2,1)}, u32[]{:S(2)}, u32[]{:S(2)}) async-start(bf16[16,2,8,6,96]{4,2,3,1,0:T(8,128)(2,1)} %copy.201), calls=%async_computation.6 | async-start | bytes 786432 | tf_op jit(solution)/shard_map/all_to_all | solution.py:83
  138.6 18.8 %all-to-all-start.9 = ((bf16[16,2,6144]{2,1,0:T(2,128)(2,1)}), bf16[16,2,6144]{2,1,0:T(2,128)(2,1)}, u32[]{:S(2)}, u32[]{:S(2)}) async-start(bf16[16,2,6144]{2,1,0:T(2,128)(2,1)} %reshape.295), calls=%async_computation.9 | async-start | bytes 786432 | tf_op jit(solution)/shard_map/all_to_all | solution.py:79
  155.6 11.4 %copy-start.31 = (bf16[6,96,128]{2,1,0:T(8,128)(2,1)}, bf16[6,96,128]{2,1,0:T(8,128)(2,1)S(1)}, u32[]{:S(2)}) copy-start(bf16[6,96,128]{2,1,0:T(8,128)(2,1)S(1)} %multiply_convert_fusion.7) | copy-start | bytes 442372
  157.4 15.0 %all-to-all-start.7 = ((bf16[16,1,8,6,96]{4,2,3,1,0:T(8,128)(2,1)}), bf16[16,1,8,6,96]{4,2,3,1,0:T(8,128)(2,1)}, u32[]{:S(2)}, u32[]{:S(2)}) async-start(bf16[16,1,8,6,96]{4,2,3,1,0:T(8,128)(2,1)} %copy.209), calls=%async_computation.7 | async-start | bytes 393216 | tf_op jit(solution)/shard_map/all_to_all | solution.py:83
  167.0 4.4 %copy-start.15 = (bf16[6,96,128]{2,1,0:T(8,128)(2,1)S(1)}, bf16[6,96,128]{2,1,0:T(8,128)(2,1)}, u32[]{:S(2)}) copy-start(bf16[6,96,128]{2,1,0:T(8,128)(2,1)} %copy-done.14) | copy-start | bytes 442372
  167.0 4.4 %copy-start.39 = (bf16[6,96,128]{2,1,0:T(8,128)(2,1)S(1)}, bf16[6,96,128]{2,1,0:T(8,128)(2,1)}, u32[]{:S(2)}) copy-start(bf16[6,96,128]{2,1,0:T(8,128)(2,1)} %get-tuple-element.68) | copy-start | bytes 442372
  169.7 4.9 %copy-start.19 = (bf16[16,1,8,6,96]{4,2,3,1,0:T(8,128)(2,1)S(1)}, bf16[16,1,8,6,96]{4,2,3,1,0:T(8,128)(2,1)}, u32[]{:S(2)}) copy-start(bf16[16,1,8,6,96]{4,2,3,1,0:T(8,128)(2,1)} %copy-done.18) | copy-start | bytes 442372
  175.1 7.9 %copy-start.52 = (bf16[128,128]{1,0:T(8,128)(2,1)S(1)}, bf16[128,128]{1,0:T(8,128)(2,1)}, u32[]{:S(2)}) copy-start(bf16[128,128]{1,0:T(8,128)(2,1)} %fusion.36) | copy-start | bytes 98308
  175.2 8.6 %copy-start.13 = (bf16[6,96,128]{2,1,0:T(8,128)(2,1)S(1)}, bf16[6,96,128]{2,1,0:T(8,128)(2,1)}, u32[]{:S(2)}) copy-start(bf16[6,96,128]{2,1,0:T(8,128)(2,1)} %copy-done.12) | copy-start | bytes 442372
  175.2 8.6 %copy-start.26 = (bf16[6,96,128]{2,1,0:T(8,128)(2,1)S(1)}, bf16[6,96,128]{2,1,0:T(8,128)(2,1)}, u32[]{:S(2)}) copy-start(bf16[6,96,128]{2,1,0:T(8,128)(2,1)} %get-tuple-element.46) | copy-start | bytes 442372
  176.0 16.3 %all-to-all-start.8 = ((bf16[16,2,8,6,96]{4,2,3,1,0:T(8,128)(2,1)}), bf16[16,2,8,6,96]{4,2,3,1,0:T(8,128)(2,1)S(1)}, u32[]{:S(2)}, u32[]{:S(2)}) async-start(bf16[16,2,8,6,96]{4,2,3,1,0:T(8,128)(2,1)} %copy.216), calls=%async_computation.8 | async-start | bytes 786432 | tf_op jit(solution)/shard_map/all_to_all | solution.py:83
  194.9 10.5 %copy-start.24 = (bf16[6,96,128]{2,1,0:T(8,128)(2,1)}, bf16[6,96,128]{2,1,0:T(8,128)(2,1)S(1)}, u32[]{:S(2)}) copy-start(bf16[6,96,128]{2,1,0:T(8,128)(2,1)S(1)} %fusion.72) | copy-start | bytes 442372
  205.4 11.9 %all-to-all-start.10 = ((bf16[16,6,6,128]{3,2,1,0:T(8,128)(2,1)}), bf16[16,6,6,128]{3,2,1,0:T(8,128)(2,1)S(1)}, u32[]{:S(2)}, u32[]{:S(2)}) async-start(bf16[16,6,6,128]{3,2,1,0:T(8,128)(2,1)} %constant_dynamic-update-slice_fusion), calls=%async_computation.10 | async-start | bytes 393216 | tf_op jit(solution)/shard_map/all_to_all | solution.py:12
  239.9 4.7 %copy-start.3 = (bf16[64,6,256]{2,0,1:T(8,128)(2,1)S(1)}, bf16[64,6,256]{2,0,1:T(8,128)(2,1)}, u32[]{:S(2)}) copy-start(bf16[64,6,256]{2,0,1:T(8,128)(2,1)} %param.10) | copy-start | bytes 589828
  239.9 4.7 %copy-start.50 = (bf16[256,64]{0,1:T(8,128)(2,1)S(1)}, bf16[256,64]{0,1:T(8,128)(2,1)}, u32[]{:S(2)}) copy-start(bf16[256,64]{0,1:T(8,128)(2,1)} %param.11) | copy-start | bytes 98308
  239.9 4.7 %copy-start.57 = (f32[64,6]{0,1:T(8,128)S(1)}, f32[64,6]{0,1:T(8,128)}, u32[]{:S(2)}) copy-start(f32[64,6]{0,1:T(8,128)} %copy-done.56) | copy-start | bytes 4612
  239.9 4.7 %copy-start.65 = (f32[64,6]{0,1:T(8,128)S(1)}, f32[64,6]{0,1:T(8,128)}, u32[]{:S(2)}) copy-start(f32[64,6]{0,1:T(8,128)} %copy-done.64) | copy-start | bytes 4612
  240.9 16.2 %all-to-all-start.12 = ((bf16[16,176,128]{2,1,0:T(8,128)(2,1)}), bf16[16,176,128]{2,1,0:T(8,128)(2,1)S(1)}, u32[]{:S(2)}, u32[]{:S(2)}) async-start(bf16[16,176,128]{2,1,0:T(8,128)(2,1)} %broadcast_in_dim.8), calls=%async_computation.12 | async-start | bytes 1441792 | tf_op jit(solution)/shard_map/all_to_all | solution.py:79
  (48 other events, 63.5 us)
